TPU v7x, 32 devices: a whole 2x2x4 slice. The times are simulated.
32 devices in a mesh: mem: 16 (over z, y, x), rep: 2 (over core).
Axes of the slice: x: 2, y: 2, z: 4, core: 2. Of those that a mesh axis runs over, the one named last changes fastest.
Arguments:
- particle_vectors: bfloat16 [64, 131072], P('mem', 'rep'), may hold values from -6 to 6
- observed: bfloat16 [64, 131072], P('mem', 'rep'), may hold values from -24 to 24
- precision: float32 [131072], P('rep'), may hold values from 0.5 to 240, as said below
- entry_projection_matrix: bfloat16 [2, 256, 1024], replicated, may hold values from -0.375 to 0.375
- entry_offsets: float32 [2, 1024], replicated, may hold values from -3 to 3
- exit_projection_matrix: bfloat16 [2, 1024, 256], replicated, may hold values from -0.1875 to 0.1875
- exit_offsets: float32 [2, 256], replicated, may hold values from -3 to 3
Outputs:
- updated: bfloat16 [64, 131072], P('mem', 'rep')
Inputs may be any that keep to these rules, and one draw needn't show every extreme that they name: `precision`: positive precisions.
All inputs are finite; a program needn't handle non-finite values.
Results may differ from a plain program's by a relative error of at most 0.0065.
Values may be sent and summed in bfloat16 or wider, within the bound.
No kernel may reach another device: no remote copies, remote signals or barrier semaphores. Data moves between devices by JAX's collectives and lax.ppermute only.
A program may use at most 64 MiB of HBM per device.

v0:
```python
import jax
import jax.numpy as jnp
from jax import lax
from jax.sharding import PartitionSpec as P

PW = 256
LAYERS = 2


def contract(left, right):
    return lax.dot_general(
        left, right, (((1,), (1,)), ((), ())), preferred_element_type=jnp.float32
    )


def body(
    particle_vectors,
    observed,
    precision,
    entry_projection_matrix,
    entry_offsets,
    exit_projection_matrix,
    exit_offsets,
):
    owned, local_width = particle_vectors.shape
    stream = particle_vectors.reshape(owned * local_width // PW, PW)
    for layer in range(LAYERS):
        pre = (
            jnp.dot(stream, entry_projection_matrix[layer], preferred_element_type=jnp.float32)
            + entry_offsets[layer]
        )
        hidden = jax.nn.silu(pre).astype(jnp.bfloat16)
        stream = (
            stream.astype(jnp.float32)
            + jnp.dot(hidden, exit_projection_matrix[layer], preferred_element_type=jnp.float32)
            + exit_offsets[layer]
        ).astype(jnp.bfloat16)
    particle_outcomes = stream.reshape(owned, local_width)
    resid = (observed.astype(jnp.float32) - particle_outcomes.astype(jnp.float32)).astype(
        jnp.bfloat16
    )
    resid_wide = resid.astype(jnp.float32)
    mem_count = lax.axis_size("mem")
    member_total = owned * mem_count
    state_total = local_width * lax.axis_size("rep")
    misfit_local = jnp.sum(resid_wide * resid_wide * precision)
    damping = lax.psum(misfit_local, ("mem", "rep")) / (member_total * state_total) + 1e-06
    own_states, own_preds, own_resid = (
        lax.all_to_all(particle_vectors, "mem", split_axis=1, concat_axis=0, tiled=True),
        lax.all_to_all(particle_outcomes, "mem", split_axis=1, concat_axis=0, tiled=True),
        lax.all_to_all(resid, "mem", split_axis=1, concat_axis=0, tiled=True),
    )
    block_width = own_states.shape[1]
    prec_block = lax.dynamic_slice_in_dim(
        precision, lax.axis_index("mem") * block_width, block_width
    )
    pred_wide = own_preds.astype(jnp.float32)
    pred_dev = (pred_wide - jnp.mean(pred_wide, axis=0)).astype(jnp.bfloat16)
    state_wide = own_states.astype(jnp.float32)
    state_dev = (state_wide - jnp.mean(state_wide, axis=0)).astype(jnp.bfloat16)
    weighted = (pred_dev.astype(jnp.float32) * prec_block).astype(jnp.bfloat16)
    gram = lax.psum(contract(weighted, pred_dev), ("mem", "rep")) / state_total
    cross = (
        lax.psum_scatter(
            contract(own_resid, weighted), ("mem", "rep"), scatter_dimension=0, tiled=True
        )
        / state_total
    )
    kmat = gram + damping * jnp.eye(member_total, dtype=jnp.float32)
    factor = jnp.linalg.cholesky(kmat)
    middle = jax.scipy.linalg.solve_triangular(factor, cross.T, lower=True)
    solved = jax.scipy.linalg.solve_triangular(factor, middle, lower=True, trans="T")
    mixing = solved.T.astype(jnp.bfloat16)
    fresh = (
        state_wide
        + jnp.dot(
            lax.all_gather(mixing, ("mem", "rep"), axis=0, tiled=True),
            state_dev,
            preferred_element_type=jnp.float32,
        )
    ).astype(jnp.bfloat16)
    return lax.all_to_all(fresh, "mem", split_axis=0, concat_axis=1, tiled=True)


def solution(mesh):
    placed = (P("mem", "rep"), P("mem", "rep"), P("rep"), P(), P(), P(), P())
    return jax.shard_map(
        body, mesh=mesh, in_specs=placed, out_specs=P("mem", "rep"), check_vma=False
    )
```

profile of v0, /device:TPU:0, one launch (start us, length us, event | category | flops | bytes accessed | tf_op | source)
XLA Modules:
  0.0 171.0 jit_solution(16117873625604666661)
XLA Ops:
  0.0 0.8 fusion.32
  0.8 0.8 fusion.33
  1.6 1.4 reshape.69
  3.0 2.5 %fusion.3 = bf16[1024,256]{1,0:T(8,128)(2,1)S(1)} fusion(bf16[1024,256]{1,0:T(8,128)(2,1)S(1)} %reshape.69, f32[1024]{0:T(1024)S(1)} %bitcast.55, f32[256]{0:T(256)S(1)} %bitcast.57, bf16[2,1024,256]{2,1,0:T(8,128)(2,1)S(1)} %copy-done.2, bf16[2,256,1024]{2,1,0:T(8,128)(2,1)} %param.10), kind=kOutput, calls=%fused_computation.12 | convolution fusion | flops 1081081856 | bytes 2626560 | tf_op jit(solution)/shard_map/dot_general | solution.py:35
  5.5 2.5 %fusion.4 = bf16[1024,256]{1,0:T(8,128)(2,1)S(1)} fusion(bf16[1024,256]{1,0:T(8,128)(2,1)S(1)} %fusion.3, f32[1024]{0:T(1024)S(1)} %bitcast.54, f32[256]{0:T(256)S(1)} %bitcast.56, bf16[2,1024,256]{2,1,0:T(8,128)(2,1)S(1)} %copy-done.2, bf16[2,256,1024]{2,1,0:T(8,128)(2,1)} %param.10), kind=kOutput, calls=%fused_computation.13 | convolution fusion | flops 1081081856 | bytes 2626560 | tf_op jit(solution)/shard_map/dot_general | solution.py:35
  8.0 0.2 all_to_all.50
  8.2 1.2 copy.17
  9.4 8.3 %all-to-all-start.1 = ((bf16[4,16,4096]{2,0,1:T(4,128)(2,1)}), bf16[4,16,4096]{2,0,1:T(4,128)(2,1)S(1)}, u32[]{:S(2)}, u32[]{:S(2)}) async-start(bf16[4,16,4096]{2,0,1:T(4,128)(2,1)} %copy.17), calls=%async_computation.1 | async-start | bytes 1048576 | tf_op jit(solution)/shard_map/all_to_all | solution.py:50
  17.8 0.5 reshape.71
  18.3 0.5 copy-done
  18.9 1.9 %multiply_reduce_fusion = (f32[]{:T(128)}, bf16[4,65536]{1,0:T(4,128)(2,1)}) fusion(f32[65536]{0:T(1024)S(1)} %copy-done.1, f32[4,65536]{1,0:T(4,128)S(1)} %reshape.71, bf16[4,65536]{1,0:T(4,128)(2,1)S(1)} %copy-done), kind=kLoop, calls=%fused_computation.18 | loop fusion | flops 1835007 | bytes 2359300 | tf_op jit(solution)/shard_map/reduce_sum | solution.py:46
  20.7 12.1 %all-to-all-done.1 = bf16[4,16,4096]{2,0,1:T(4,128)(2,1)S(1)} async-done(((bf16[4,16,4096]{2,0,1:T(4,128)(2,1)}), bf16[4,16,4096]{2,0,1:T(4,128)(2,1)S(1)}, u32[]{:S(2)}, u32[]{:S(2)}) %all-to-all-start.1) | async-done | bytes 524320 | tf_op jit(solution)/shard_map/all_to_all | solution.py:50
  32.8 3.9 %all-to-all-start.2 = ((bf16[4,16,4096]{2,0,1:T(4,128)(2,1)}), bf16[4,16,4096]{2,0,1:T(4,128)(2,1)S(1)}, u32[]{:S(2)}, u32[]{:S(2)}) async-start(bf16[4,16,4096]{2,0,1:T(4,128)(2,1)} %bitcast.14), calls=%async_computation.2 | async-start | bytes 1048576 | tf_op jit(solution)/shard_map/all_to_all | solution.py:51
  36.8 0.2 convert_reduce_fusion.1
  37.1 0.5 multiply_convert_fusion.2
  37.9 13.4 %all-to-all-done.2 = bf16[4,16,4096]{2,0,1:T(4,128)(2,1)S(1)} async-done(((bf16[4,16,4096]{2,0,1:T(4,128)(2,1)}), bf16[4,16,4096]{2,0,1:T(4,128)(2,1)S(1)}, u32[]{:S(2)}, u32[]{:S(2)}) %all-to-all-start.2) | async-done | bytes 524320 | tf_op jit(solution)/shard_map/all_to_all | solution.py:51
  51.2 3.9 %all-to-all-start = ((bf16[4,16,4096]{2,0,1:T(4,128)(2,1)}), bf16[4,16,4096]{2,0,1:T(4,128)(2,1)S(1)}, u32[]{:S(2)}, u32[]{:S(2)}) async-start(bf16[4,16,4096]{2,0,1:T(4,128)(2,1)} %bitcast), calls=%async_computation | async-start | bytes 1048576 | tf_op jit(solution)/shard_map/all_to_all | solution.py:49
  55.2 0.3 fusion.34
  55.5 0.3 fusion.35
  55.8 42.0 %all-reduce.1 = (f32[64,64]{1,0:T(8,128)S(1)}, f32[]{:T(128)}, f32[64,64]{1,0:T(8,128)S(1)}) all-reduce(f32[64,64]{1,0:T(8,128)S(1)} %fusion.34, f32[]{:T(128)} %get-tuple-element.8, f32[64,64]{1,0:T(8,128)S(1)} %fusion.35), channel_id=1, replica_groups=mesh['mem'=16,'rep'=2] {'mem','rep'}, use_global_device_ids=true, to_apply=%region_1.2 | all-reduce | flops 8193 | bytes 65544 | tf_op jit(solution)/shard_map/psum | solution.py:62
  98.6 5.8 %cholesky.16 = f32[64,64]{1,0:T(8,128)S(1)} custom-call(f32[64,64]{1,0:T(8,128)S(1)} %fusion.25), custom_call_target="Cholesky" | custom-call | tf_op jit(solution)/shard_map/jit(cholesky)/cholesky | solution.py:70
  104.5 0.6 compare_reduce_fusion
  105.2 0.7 fusion.21
  105.8 4.9 %custom-call.10 = f32[1,64,64]{1,2,0:T(8,128)S(1)} custom-call(f32[1,64,64]{2,1,0:T(8,128)S(1)} %fusion.21), custom_call_target="InvertDiagBlocksLowerTriangular" | custom-call | tf_op jit(solution)/shard_map/jit(_solve_triangular)/triangular_solve | solution.py:72
  110.9 0.2 fusion.5
  111.0 39.9 %all-gather = bf16[32,2,64]{2,1,0:T(2,128)(2,1)S(1)} all-gather(bf16[1,2,64]{2,1,0:T(2,128)(2,1)S(1)} %fusion.5), channel_id=1, replica_groups=mesh['mem'=16,'rep'=2] {'mem','rep'}, dimensions={0}, use_global_device_ids=true | all-gather | bytes 8448 | tf_op jit(solution)/shard_map/all_gather | solution.py:77
  151.0 0.4 reshape.70
  151.4 0.2 convert_reduce_fusion
  151.6 0.3 fusion
  151.9 0.2 all_to_all.56
  152.1 18.1 %all_to_all.64 = bf16[16,4,4096]{2,1,0:T(4,128)(2,1)S(1)} all-to-all(bf16[16,4,4096]{2,1,0:T(4,128)(2,1)S(1)} %all_to_all.56), channel_id=1, replica_groups=mesh['mem'=16,'rep'=2] {'mem'}, dimensions={0} | all-to-all | bytes 1048576 | tf_op jit(solution)/shard_map/all_to_all | solution.py:82
  170.2 0.8 copy.22
  (19 shorter events, 0.8 us)
Async XLA Ops:
  0.0 3.0 %copy-start.2 = (bf16[2,1024,256]{2,1,0:T(8,128)(2,1)S(1)}, bf16[2,1024,256]{2,1,0:T(8,128)(2,1)}, u32[]{:S(2)}) copy-start(bf16[2,1024,256]{2,1,0:T(8,128)(2,1)} %param.12) | copy-start | bytes 3145732
  9.4 23.4 %all-to-all-start.1 = ((bf16[4,16,4096]{2,0,1:T(4,128)(2,1)}), bf16[4,16,4096]{2,0,1:T(4,128)(2,1)S(1)}, u32[]{:S(2)}, u32[]{:S(2)}) async-start(bf16[4,16,4096]{2,0,1:T(4,128)(2,1)} %copy.17), calls=%async_computation.1 | async-start | bytes 1048576 | tf_op jit(solution)/shard_map/all_to_all | solution.py:50
  17.8 1.0 copy-start
  17.8 1.1 copy-start.1
  20.7 16.3 %dynamic-slice-start = ((f32[65536]{0:T(1024)}, s32[]{:T(128)}), f32[4096]{0:T(1024)S(1)}, s32[]{:S(2)}) async-start(f32[65536]{0:T(1024)} %param.9, s32[]{:T(128)} %select_n.7), calls=%async_computation.4 | async-start | bytes 33280 | tf_op jit(solution)/shard_map/dynamic_slice | solution.py:54
  32.8 18.4 %all-to-all-start.2 = ((bf16[4,16,4096]{2,0,1:T(4,128)(2,1)}), bf16[4,16,4096]{2,0,1:T(4,128)(2,1)S(1)}, u32[]{:S(2)}, u32[]{:S(2)}) async-start(bf16[4,16,4096]{2,0,1:T(4,128)(2,1)} %bitcast.14), calls=%async_computation.2 | async-start | bytes 1048576 | tf_op jit(solution)/shard_map/all_to_all | solution.py:51
  51.2 99.7 %all-to-all-start = ((bf16[4,16,4096]{2,0,1:T(4,128)(2,1)}), bf16[4,16,4096]{2,0,1:T(4,128)(2,1)S(1)}, u32[]{:S(2)}, u32[]{:S(2)}) async-start(bf16[4,16,4096]{2,0,1:T(4,128)(2,1)} %bitcast), calls=%async_computation | async-start | bytes 1048576 | tf_op jit(solution)/shard_map/all_to_all | solution.py:49
where the time goes:
time: 172 us; the launch traced here: 171 us
  blocking collectives  100 us (58%)
  waiting for transfers between devices  25.5 us (15%)
  starting transfers between devices  16.2 us (9%)
  other arithmetic  15.1 us (9%)
  local copies, waits for them, and re-layouts  7.34 us (4%)
  matrix products  6.07 us (4%)
    psum x1, blocking collectives, body(): gram = lax.psum(contract(weighted, pred_dev), ('mem', 'rep')) / state_total  42 us
    all_gather x1, blocking collectives, body(): lax.all_gather(mixing, ('mem', 'rep'), axis=0, tiled=True)  39.9 us
    all_to_all x1, blocking collectives, body(): return lax.all_to_all(fresh, 'mem', split_axis=0, concat_axis=1, tiled=True)  18.1 us
    all_to_all x1, waiting for transfers between devices, body(): lax.all_to_all(resid, 'mem', split_axis=1, concat_axis=0, tiled=True)  13.4 us
    all_to_all x1, waiting for transfers between devices, body(): lax.all_to_all(particle_outcomes, 'mem', split_axis=1, concat_axis=0, til...  12.1 us
    all_to_all x1, starting transfers between devices, body(): lax.all_to_all(particle_outcomes, 'mem', split_axis=1, concat_axis=0, til...  8.34 us
    another operation x3, other arithmetic, body(): factor = jnp.linalg.cholesky(kmat)  6.52 us
    another operation x2, other arithmetic, body(): jax.scipy.linalg.solve_triangular(factor, middle, lower=True, trans='T')  5.55 us
  transfers between devices with their start and end apart: 3, of which 2 were waited for; matrix products, arithmetic and copies ran while one was open for 10% of the time, Pallas kernels for 0%

commit v1 on v0

--- a/solution.py
+++ b/solution.py
@@ -5,6 +5,12 @@
 
 PW = 256
 LAYERS = 2
+
+
+def recover_scales(x_part):
+    for t in ("rep", "mem"):
+        x_part = lax.psum(x_part, axis_name=t)
+    return x_part
 
 
 def contract(left, right):
@@ -59,7 +65,7 @@
     state_wide = own_states.astype(jnp.float32)
     state_dev = (state_wide - jnp.mean(state_wide, axis=0)).astype(jnp.bfloat16)
     weighted = (pred_dev.astype(jnp.float32) * prec_block).astype(jnp.bfloat16)
-    gram = lax.psum(contract(weighted, pred_dev), ("mem", "rep")) / state_total
+    gram = recover_scales(contract(weighted, pred_dev)) / state_total
     cross = (
         lax.psum_scatter(
             contract(own_resid, weighted), ("mem", "rep"), scatter_dimension=0, tiled=True

time: 172 us -> 239 us (1.39)
  blocking collectives: 100 us -> 181 us
  waiting for transfers between devices: 25.5 us -> 12.1 us
    psum x1 -> x3, blocking collectives: 42 us -> 122 us  [the longest x2 80.9 us: recover_scales(): x_part = lax.psum(x_part, axis_name=t)]
    all_to_all x1, waiting for transfers between devices: 13.4 us -> 0.01 us  [body(): lax.all_to_all(resid, 'mem', split_axis=1, concat_axis=0, tiled=True)]
  transfers between devices with their start and end apart: 3 -> 3, of which waited for: 2 -> 1; matrix products, arithmetic and copies ran while one was open for 10% -> 7% of each run, Pallas kernels for 0% -> 0%
where the time goes in v1:
time: 239 us; the launch traced here: 238 us
  blocking collectives  181 us (76%)
  starting transfers between devices  15.9 us (7%)
  other arithmetic  15.1 us (6%)
  waiting for transfers between devices  12.1 us (5%)
  local copies, waits for them, and re-layouts  7.34 us (3%)
  matrix products  6.07 us (3%)
    psum x2, blocking collectives, recover_scales(): x_part = lax.psum(x_part, axis_name=t)  80.9 us
    psum x1, blocking collectives, body(): lax.psum(misfit_local, ('mem', 'rep')) / (member_total * state_total)  41.4 us
    all_gather x1, blocking collectives, body(): lax.all_gather(mixing, ('mem', 'rep'), axis=0, tiled=True)  40.3 us
    all_to_all x1, blocking collectives, body(): return lax.all_to_all(fresh, 'mem', split_axis=0, concat_axis=1, tiled=True)  18.1 us
    all_to_all x1, waiting for transfers between devices, body(): lax.all_to_all(particle_outcomes, 'mem', split_axis=1, concat_axis=0, til...  12.1 us
    all_to_all x1, starting transfers between devices, body(): lax.all_to_all(particle_outcomes, 'mem', split_axis=1, concat_axis=0, til...  8.34 us
    another operation x3, other arithmetic, body(): factor = jnp.linalg.cholesky(kmat)  6.52 us
    another operation x2, other arithmetic, body(): jax.scipy.linalg.solve_triangular(factor, middle, lower=True, trans='T')  5.55 us
  transfers between devices with their start and end apart: 3, of which 1 were waited for; matrix products, arithmetic and copies ran while one was open for 7% of the time, Pallas kernels for 0%

profile of v1, /device:TPU:0, one launch (start us, length us, event | category | flops | bytes accessed | tf_op | source)
XLA Modules:
  0.0 238.0 jit_solution(13207978428760311363)
XLA Ops:
  0.0 0.8 fusion.32
  0.8 0.8 fusion.33
  1.6 1.4 reshape.69
  3.0 2.5 %fusion.3 = bf16[1024,256]{1,0:T(8,128)(2,1)S(1)} fusion(bf16[1024,256]{1,0:T(8,128)(2,1)S(1)} %reshape.69, f32[1024]{0:T(1024)S(1)} %bitcast.55, f32[256]{0:T(256)S(1)} %bitcast.57, bf16[2,1024,256]{2,1,0:T(8,128)(2,1)S(1)} %copy-done.2, bf16[2,256,1024]{2,1,0:T(8,128)(2,1)} %param.10), kind=kOutput, calls=%fused_computation.12 | convolution fusion | flops 1081081856 | bytes 2626560 | tf_op jit(solution)/shard_map/dot_general | solution.py:41
  5.5 2.5 %fusion.4 = bf16[1024,256]{1,0:T(8,128)(2,1)S(1)} fusion(bf16[1024,256]{1,0:T(8,128)(2,1)S(1)} %fusion.3, f32[1024]{0:T(1024)S(1)} %bitcast.54, f32[256]{0:T(256)S(1)} %bitcast.56, bf16[2,1024,256]{2,1,0:T(8,128)(2,1)S(1)} %copy-done.2, bf16[2,256,1024]{2,1,0:T(8,128)(2,1)} %param.10), kind=kOutput, calls=%fused_computation.13 | convolution fusion | flops 1081081856 | bytes 2626560 | tf_op jit(solution)/shard_map/dot_general | solution.py:41
  8.0 0.2 all_to_all.50
  8.2 1.2 copy.17
  9.4 8.3 %all-to-all-start.1 = ((bf16[4,16,4096]{2,0,1:T(4,128)(2,1)}), bf16[4,16,4096]{2,0,1:T(4,128)(2,1)S(1)}, u32[]{:S(2)}, u32[]{:S(2)}) async-start(bf16[4,16,4096]{2,0,1:T(4,128)(2,1)} %copy.17), calls=%async_computation.1 | async-start | bytes 1048576 | tf_op jit(solution)/shard_map/all_to_all | solution.py:56
  17.8 0.5 reshape.71
  18.3 0.5 copy-done
  18.9 1.9 multiply_reduce_fusion
  20.7 12.1 %all-to-all-done.1 = bf16[4,16,4096]{2,0,1:T(4,128)(2,1)S(1)} async-done(((bf16[4,16,4096]{2,0,1:T(4,128)(2,1)}), bf16[4,16,4096]{2,0,1:T(4,128)(2,1)S(1)}, u32[]{:S(2)}, u32[]{:S(2)}) %all-to-all-start.1) | async-done | bytes 524320 | tf_op jit(solution)/shard_map/all_to_all | solution.py:56
  32.8 3.9 %all-to-all-start.2 = ((bf16[4,16,4096]{2,0,1:T(4,128)(2,1)}), bf16[4,16,4096]{2,0,1:T(4,128)(2,1)S(1)}, u32[]{:S(2)}, u32[]{:S(2)}) async-start(bf16[4,16,4096]{2,0,1:T(4,128)(2,1)} %bitcast.14), calls=%async_computation.2 | async-start | bytes 1048576 | tf_op jit(solution)/shard_map/all_to_all | solution.py:57
  36.8 0.2 convert_reduce_fusion.1
  37.1 0.5 multiply_convert_fusion.2
  37.9 0.3 fusion.34
  38.2 3.4 %psum.21 = f32[64,64]{1,0:T(8,128)S(1)} all-reduce(f32[64,64]{1,0:T(8,128)S(1)} %fusion.34), channel_id=1, replica_groups=mesh['mem'=16,'rep'=2] {'rep'}, use_global_device_ids=true, to_apply=%region_1.2 | all-reduce | flops 4096 | bytes 32768 | tf_op jit(solution)/shard_map/psum | solution.py:12
  41.6 77.5 %psum.22 = f32[64,64]{1,0:T(8,128)S(1)} all-reduce(f32[64,64]{1,0:T(8,128)S(1)} %psum.21), channel_id=1, replica_groups=mesh['mem'=16,'rep'=2] {'mem'}, use_global_device_ids=true, to_apply=%region_2.3 | all-reduce | flops 4096 | bytes 32768 | tf_op jit(solution)/shard_map/psum | solution.py:12
  119.0 3.6 %all-to-all-start = ((bf16[4,16,4096]{2,0,1:T(4,128)(2,1)}), bf16[4,16,4096]{2,0,1:T(4,128)(2,1)S(1)}, u32[]{:S(2)}, u32[]{:S(2)}) async-start(bf16[4,16,4096]{2,0,1:T(4,128)(2,1)} %bitcast), calls=%async_computation | async-start | bytes 1048576 | tf_op jit(solution)/shard_map/all_to_all | solution.py:55
  122.8 0.3 fusion.35
  123.0 41.4 %all-reduce.1 = (f32[]{:T(128)}, f32[64,64]{1,0:T(8,128)S(1)}) all-reduce(f32[]{:T(128)} %get-tuple-element.7, f32[64,64]{1,0:T(8,128)S(1)} %fusion.35), channel_id=1, replica_groups=mesh['mem'=16,'rep'=2] {'mem','rep'}, use_global_device_ids=true, to_apply=%region_4.5 | all-reduce | flops 4097 | bytes 32776 | tf_op jit(solution)/shard_map/psum | solution.py:53
  165.2 5.8 %cholesky.16 = f32[64,64]{1,0:T(8,128)S(1)} custom-call(f32[64,64]{1,0:T(8,128)S(1)} %fusion.25), custom_call_target="Cholesky" | custom-call | tf_op jit(solution)/shard_map/jit(cholesky)/cholesky | solution.py:76
  171.1 0.6 compare_reduce_fusion
  171.7 0.7 fusion.21
  172.4 4.9 %custom-call.10 = f32[1,64,64]{1,2,0:T(8,128)S(1)} custom-call(f32[1,64,64]{2,1,0:T(8,128)S(1)} %fusion.21), custom_call_target="InvertDiagBlocksLowerTriangular" | custom-call | tf_op jit(solution)/shard_map/jit(_solve_triangular)/triangular_solve | solution.py:78
  177.6 40.3 %all-gather = bf16[32,2,64]{2,1,0:T(2,128)(2,1)S(1)} all-gather(bf16[1,2,64]{2,1,0:T(2,128)(2,1)S(1)} %fusion.5), channel_id=1, replica_groups=mesh['mem'=16,'rep'=2] {'mem','rep'}, dimensions={0}, use_global_device_ids=true | all-gather | bytes 8448 | tf_op jit(solution)/shard_map/all_gather | solution.py:83
  218.0 0.4 reshape.70
  218.4 0.2 convert_reduce_fusion
  218.6 0.3 fusion
  218.9 0.2 all_to_all.56
  219.1 18.1 %all_to_all.64 = bf16[16,4,4096]{2,1,0:T(4,128)(2,1)S(1)} all-to-all(bf16[16,4,4096]{2,1,0:T(4,128)(2,1)S(1)} %all_to_all.56), channel_id=1, replica_groups=mesh['mem'=16,'rep'=2] {'mem'}, dimensions={0} | all-to-all | bytes 1048576 | tf_op jit(solution)/shard_map/all_to_all | solution.py:88
  237.2 0.8 copy.22
  (21 shorter events, 1.0 us)
Async XLA Ops:
  0.0 3.0 %copy-start.2 = (bf16[2,1024,256]{2,1,0:T(8,128)(2,1)S(1)}, bf16[2,1024,256]{2,1,0:T(8,128)(2,1)}, u32[]{:S(2)}) copy-start(bf16[2,1024,256]{2,1,0:T(8,128)(2,1)} %param.12) | copy-start | bytes 3145732
  9.4 23.4 %all-to-all-start.1 = ((bf16[4,16,4096]{2,0,1:T(4,128)(2,1)}), bf16[4,16,4096]{2,0,1:T(4,128)(2,1)S(1)}, u32[]{:S(2)}, u32[]{:S(2)}) async-start(bf16[4,16,4096]{2,0,1:T(4,128)(2,1)} %copy.17), calls=%async_computation.1 | async-start | bytes 1048576 | tf_op jit(solution)/shard_map/all_to_all | solution.py:56
  17.8 1.0 copy-start
  17.8 1.1 copy-start.1
  20.7 16.3 %dynamic-slice-start = ((f32[65536]{0:T(1024)}, s32[]{:T(128)}), f32[4096]{0:T(1024)S(1)}, s32[]{:S(2)}) async-start(f32[65536]{0:T(1024)} %param.9, s32[]{:T(128)} %select_n.7), calls=%async_computation.4 | async-start | bytes 33280 | tf_op jit(solution)/shard_map/dynamic_slice | solution.py:60
  32.8 86.2 %all-to-all-start.2 = ((bf16[4,16,4096]{2,0,1:T(4,128)(2,1)}), bf16[4,16,4096]{2,0,1:T(4,128)(2,1)S(1)}, u32[]{:S(2)}, u32[]{:S(2)}) async-start(bf16[4,16,4096]{2,0,1:T(4,128)(2,1)} %bitcast.14), calls=%async_computation.2 | async-start | bytes 1048576 | tf_op jit(solution)/shard_map/all_to_all | solution.py:57
  119.0 98.8 %all-to-all-start = ((bf16[4,16,4096]{2,0,1:T(4,128)(2,1)}), bf16[4,16,4096]{2,0,1:T(4,128)(2,1)S(1)}, u32[]{:S(2)}, u32[]{:S(2)}) async-start(bf16[4,16,4096]{2,0,1:T(4,128)(2,1)} %bitcast), calls=%async_computation | async-start | bytes 1048576 | tf_op jit(solution)/shard_map/all_to_all | solution.py:55
